TPU v7x, 512 devices: a whole 4x4x16 slice. The times are simulated.
512 devices in a mesh: row: 32 (over z_hi, x, y), col: 16 (over z_lo, core).
Axes of the slice: x: 4, y: 4, z: 16 (z_hi: 2, z_lo: 8; z = z_hi * 8 + z_lo), core: 2. Of those that a mesh axis runs over, the one named last changes fastest.
Arguments:
- replicas: bfloat16 [10240, 40960], P('row', 'col'), may hold values from -24 to 24
- factor_seeds: int32 [8, 8, 2, 2], replicated, may hold values from 0 to 8190
- edge_counts: int32 [8, 8, 2], replicated, may hold values from 1 to 4
Outputs:
- update: float32 [10240, 40960], P('row', 'col')
All inputs are finite; a program needn't handle non-finite values.
Results may differ from a plain program's by a relative error of at most 0.0003.
Values sent between devices are 32-bit elements; how exact they have to be, the bound alone decides.
A program may use at most 64 MiB of HBM per device.

v0:
```python
import jax
import jax.numpy as jnp
from jax import lax
from jax.sharding import PartitionSpec as P

ROUNDS = 2
ROW_SHARDS = 4
COL_SHARDS = 2


highest = lax.Precision.HIGHEST
epsilon = 1e-06


def swapped(value, axis, apart):
    return lax.ppermute(value, axis, [(i, i ^ 1 << apart) for i in range(lax.axis_size(axis))])


def from_behind(value, axis, by):
    length = lax.axis_size(axis)
    return lax.ppermute(value, axis, [(i, (i + by) % length) for i in range(length)])


def start_factors(my_seeds, first_column, width):
    column = first_column + jnp.arange(width, dtype=jnp.int32)
    square = column * column % 8191
    residue = (square * (my_seeds[..., None] + 1) + column * 17) % 8191
    return residue.astype(jnp.float32) * (2.0 / 8191.0) - 1.0


def column_total(values):
    values = values + swapped(values, "col", 0)
    return values


def inner_total(values):
    for bit_level in range(ROW_SHARDS.bit_length() - 1):
        values = values + swapped(values, "row", bit_level)
    return values


def projection_total(values):
    for bit_level in range(ROW_SHARDS.bit_length() - 1):
        values = values + swapped(values, "row", bit_level)
    return values


def image_neighbours(stacked):
    from_below = from_behind(stacked[1], "row", -ROW_SHARDS)
    from_above = from_behind(stacked[0], "row", ROW_SHARDS)
    from_right = from_behind(stacked[3], "col", -COL_SHARDS)
    from_left = from_behind(stacked[2], "col", COL_SHARDS)
    return jnp.stack([from_below, from_above, from_right, from_left])


def projection_neighbours(stacked):
    from_below = from_behind(stacked[1], "row", -ROW_SHARDS)
    from_above = from_behind(stacked[0], "row", ROW_SHARDS)
    from_right = from_behind(stacked[3], "col", -COL_SHARDS)
    from_left = from_behind(stacked[2], "col", COL_SHARDS)
    return jnp.stack([from_below, from_above, from_right, from_left])


def orthonormal(values):
    leading = values[:, 0, :]
    second = values[:, 1, :]
    statistics = inner_total(
        jnp.stack(
            [
                jnp.sum(leading * leading, -1),
                jnp.sum(leading * second, -1),
                jnp.sum(second * second, -1),
            ]
        )
    )
    lead_root = jnp.sqrt(statistics[0] + epsilon)
    correlation = statistics[1] / lead_root
    rest_root = jnp.sqrt(statistics[2] - correlation * correlation + epsilon)
    leading = leading / lead_root[:, None]
    second = (second - correlation[:, None] * leading) / rest_root[:, None]
    return jnp.stack([leading, second], 1)


def per_device(replicas, factor_seeds, edge_counts):
    local_rows, local_cols = replicas.shape
    graph_rows, graph_cols = (factor_seeds.shape[0], factor_seeds.shape[1])
    node_row = lax.axis_index("row") // ROW_SHARDS
    node_col = lax.axis_index("col") // COL_SHARDS
    first_column = lax.axis_index("col") % COL_SHARDS * local_cols
    above_row = (node_row + graph_rows - 1) % graph_rows
    left_col = (node_col + graph_cols - 1) % graph_cols
    my_seeds = jnp.stack(
        [
            factor_seeds[node_row, node_col, 0],
            factor_seeds[above_row, node_col, 0],
            factor_seeds[node_row, node_col, 1],
            factor_seeds[node_row, left_col, 1],
        ]
    )
    counts = jnp.stack(
        [
            edge_counts[node_row, node_col, 0],
            edge_counts[above_row, node_col, 0],
            edge_counts[node_row, node_col, 1],
            edge_counts[node_row, left_col, 1],
        ]
    )
    scaling = -(counts.astype(jnp.float32) / 16.0)
    factors = start_factors(my_seeds, first_column, local_cols)
    edge_rows = factors.shape[0] * factors.shape[1]
    update = None
    for round_index in range(ROUNDS):
        flat_factors = factors.reshape(edge_rows, local_cols)
        images = jnp.einsum(
            "fm,km->fk",
            flat_factors,
            replicas,
            precision=highest,
            preferred_element_type=jnp.float32,
        )
        if update is not None:
            images = images + jnp.einsum("fm,km->fk", flat_factors, update, precision=highest)
        images = column_total(images).reshape(factors.shape[0], factors.shape[1], local_rows)
        directions = orthonormal(images - image_neighbours(images))
        flat_directions = directions.reshape(edge_rows, local_rows)
        projections = jnp.einsum(
            "fk,km->fm",
            flat_directions,
            replicas,
            precision=highest,
            preferred_element_type=jnp.float32,
        )
        if update is not None:
            projections = projections + jnp.einsum(
                "fk,km->fm", flat_directions, update, precision=highest
            )
        projections = projections.reshape(factors.shape)
        factors = projection_total(projections + projection_neighbours(projections))
        weighted = (scaling[:, None, None] * factors).reshape(edge_rows, local_cols)
        correction = jnp.einsum("fk,fm->km", flat_directions, weighted, precision=highest)
        update = correction if update is None else update + correction
    return update


def solution(mesh):
    in_specs = (P("row", "col"), P(), P())
    out_specs = P("row", "col")
    return jax.shard_map(
        per_device, mesh=mesh, in_specs=in_specs, out_specs=out_specs, check_vma=False
    )
```

profile of v0, /device:TPU:16, one launch (start us, length us, event | category | flops | bytes accessed | tf_op | source)
XLA Modules:
  0.0 221.4 jit_solution(8529706724505793027)
XLA Ops:
  6.0 17.9 %collective-permute-start.1 = (f32[2,320]{1,0:T(2,128)S(1)}, f32[2,320]{1,0:T(2,128)S(1)}, u32[]{:S(2)}, u32[]{:S(2)}) collective-permute-start(f32[2,320]{1,0:T(2,128)S(1)} %get-tuple-element.35), channel_id=1, source_target_pairs={{0,448},{16,464},{32,480},{48,496},{64,0},{80,16},{96,32},{112,48}... | collective-permute-start | bytes 7688 | tf_op jit(solution)/shard_map/ppermute | solution.py:21
  23.9 2.9 %collective-permute-start.4 = (f32[2,320]{1,0:T(2,128)S(1)}, f32[2,320]{1,0:T(2,128)S(1)}, u32[]{:S(2)}, u32[]{:S(2)}) collective-permute-start(f32[2,320]{1,0:T(2,128)S(1)} %get-tuple-element.36), channel_id=1, source_target_pairs={{0,2},{1,3},{2,4},{3,5},{4,6},{5,7},{6,8},{7,9},{8,10},{9,11},{10,... | collective-permute-start | bytes 7688 | tf_op jit(solution)/shard_map/ppermute | solution.py:21
  26.9 9.5 %collective-permute-start.3 = (f32[2,320]{1,0:T(2,128)S(1)}, f32[2,320]{1,0:T(2,128)S(1)}, u32[]{:S(2)}, u32[]{:S(2)}) collective-permute-start(f32[2,320]{1,0:T(2,128)S(1)} %get-tuple-element.37), channel_id=1, source_target_pairs={{0,14},{1,15},{2,0},{3,1},{4,2},{5,3},{6,4},{7,5},{8,6},{9,7},{10,... | collective-permute-start | bytes 7688 | tf_op jit(solution)/shard_map/ppermute | solution.py:21
  38.4 14.3 %collective-permute-done.2 = f32[2,320]{1,0:T(2,128)S(1)} collective-permute-done((f32[2,320]{1,0:T(2,128)S(1)}, f32[2,320]{1,0:T(2,128)S(1)}, u32[]{:S(2)}, u32[]{:S(2)}) %collective-permute-start.2) | collective-permute-done | bytes 2592 | tf_op jit(solution)/shard_map/ppermute | solution.py:21
  52.8 3.2 %collective-permute-start.5 = (f32[3,4]{1,0:T(4,128)S(1)}, f32[3,4]{1,0:T(4,128)S(1)}, u32[]{:S(2)}, u32[]{:S(2)}) collective-permute-start(f32[3,4]{1,0:T(4,128)S(1)} %pad_maximum_fusion.2), channel_id=1, source_target_pairs={{0,16},{16,0},{32,48},{48,32},{64,80},{80,64},{96,112},{112,96},{1... | collective-permute-start | bytes 152 | tf_op jit(solution)/shard_map/ppermute | solution.py:16
  60.6 4.7 %collective-permute-done.6 = f32[3,4]{1,0:T(4,128)S(1)} collective-permute-done((f32[3,4]{1,0:T(4,128)S(1)}, f32[3,4]{1,0:T(4,128)S(1)}, u32[]{:S(2)}, u32[]{:S(2)}) %collective-permute-start.6) | collective-permute-done | bytes 80 | tf_op jit(solution)/shard_map/ppermute | solution.py:16
  70.1 10.5 %collective-permute-start.9 = (f32[2,2560]{1,0:T(2,128)S(1)}, f32[2,2560]{1,0:T(2,128)S(1)}, u32[]{:S(2)}, u32[]{:S(2)}) collective-permute-start(f32[2,2560]{1,0:T(2,128)S(1)} %get-tuple-element.29), channel_id=1, source_target_pairs={{0,14},{1,15},{2,0},{3,1},{4,2},{5,3},{6,4},{7,5},{8,6},{9,7},{10,... | collective-permute-start | bytes 61448 | tf_op jit(solution)/shard_map/ppermute | solution.py:21
  80.7 3.9 %collective-permute-start.8 = (f32[2,2560]{1,0:T(2,128)S(1)}, f32[2,2560]{1,0:T(2,128)S(1)}, u32[]{:S(2)}, u32[]{:S(2)}) collective-permute-start(f32[2,2560]{1,0:T(2,128)S(1)} %get-tuple-element.30), channel_id=1, source_target_pairs={{0,64},{16,80},{32,96},{48,112},{64,128},{80,144},{96,160},{112,17... | collective-permute-start | bytes 61448 | tf_op jit(solution)/shard_map/ppermute | solution.py:21
  84.7 12.5 %collective-permute-done.8 = f32[2,2560]{1,0:T(2,128)S(1)} collective-permute-done((f32[2,2560]{1,0:T(2,128)S(1)}, f32[2,2560]{1,0:T(2,128)S(1)}, u32[]{:S(2)}, u32[]{:S(2)}) %collective-permute-start.8) | collective-permute-done | bytes 20512 | tf_op jit(solution)/shard_map/ppermute | solution.py:21
  97.2 3.2 %collective-permute-start.11 = (f32[4,2,2560]{2,1,0:T(2,128)S(1)}, f32[4,2,2560]{2,1,0:T(2,128)S(1)}, u32[]{:S(2)}, u32[]{:S(2)}) collective-permute-start(f32[4,2,2560]{2,1,0:T(2,128)S(1)} %maximum_add_fusion), channel_id=1, source_target_pairs={{0,16},{16,0},{32,48},{48,32},{64,80},{80,64},{96,112},{112,96},{1... | collective-permute-start | bytes 245768 | tf_op jit(solution)/shard_map/ppermute | solution.py:16
  111.7 2.8 %convolution_bitcast_fusion.1 = f32[320,2560]{1,0:T(8,128)S(1)} fusion(f32[4,2,2560]{2,1,0:T(2,128)S(1)} %add.205, f32[4]{0:T(128)S(1)} %fusion.33, f32[4,1,320]{2,1,0:T(1,128)S(1)} %get-tuple-element.19, f32[4,1,320]{2,1,0:T(1,128)S(1)} %get-tuple-element.20), kind=kOutput, calls=%fused_computation.1 | convolution fusion | flops 78666240 | bytes 3368976 | tf_op jit(solution)/shard_map/fk,fm->km/dot_general | solution.py:140
  125.7 10.5 %collective-permute-start.16 = (f32[2,320]{1,0:T(2,128)S(1)}, f32[2,320]{1,0:T(2,128)S(1)}, u32[]{:S(2)}, u32[]{:S(2)}) collective-permute-start(f32[2,320]{1,0:T(2,128)S(1)} %get-tuple-element.33), channel_id=1, source_target_pairs={{0,14},{1,15},{2,0},{3,1},{4,2},{5,3},{6,4},{7,5},{8,6},{9,7},{10,... | collective-permute-start | bytes 7688 | tf_op jit(solution)/shard_map/ppermute | solution.py:21
  136.2 3.9 %collective-permute-start.15 = (f32[2,320]{1,0:T(2,128)S(1)}, f32[2,320]{1,0:T(2,128)S(1)}, u32[]{:S(2)}, u32[]{:S(2)}) collective-permute-start(f32[2,320]{1,0:T(2,128)S(1)} %get-tuple-element.34), channel_id=1, source_target_pairs={{0,64},{16,80},{32,96},{48,112},{64,128},{80,144},{96,160},{112,17... | collective-permute-start | bytes 7688 | tf_op jit(solution)/shard_map/ppermute | solution.py:21
  140.2 12.3 %collective-permute-done.15 = f32[2,320]{1,0:T(2,128)S(1)} collective-permute-done((f32[2,320]{1,0:T(2,128)S(1)}, f32[2,320]{1,0:T(2,128)S(1)}, u32[]{:S(2)}, u32[]{:S(2)}) %collective-permute-start.15) | collective-permute-done | bytes 2592 | tf_op jit(solution)/shard_map/ppermute | solution.py:21
  152.7 3.1 %collective-permute-start.18 = (f32[3,4]{1,0:T(4,128)S(1)}, f32[3,4]{1,0:T(4,128)S(1)}, u32[]{:S(2)}, u32[]{:S(2)}) collective-permute-start(f32[3,4]{1,0:T(4,128)S(1)} %pad_maximum_fusion.3), channel_id=1, source_target_pairs={{0,16},{16,0},{32,48},{48,32},{64,80},{80,64},{96,112},{112,96},{1... | collective-permute-start | bytes 152 | tf_op jit(solution)/shard_map/ppermute | solution.py:16
  160.6 4.6 %collective-permute-done.19 = f32[3,4]{1,0:T(4,128)S(1)} collective-permute-done((f32[3,4]{1,0:T(4,128)S(1)}, f32[3,4]{1,0:T(4,128)S(1)}, u32[]{:S(2)}, u32[]{:S(2)}) %collective-permute-start.19) | collective-permute-done | bytes 80 | tf_op jit(solution)/shard_map/ppermute | solution.py:16
  165.3 3.6 %fusion.49 = f32[8,2560]{1,0:T(8,128)S(1)} fusion(f32[8,320]{1,0:T(8,128)S(1)} %reshape.259, f32[320,2560]{1,0:T(8,128)} %copy-done.1), kind=kOutput, calls=%fused_computation.92 | convolution fusion | flops 78643200 | bytes 3368960 | tf_op jit(solution)/shard_map/fk,km->fm/dot_general | solution.py:134
  173.5 10.5 %collective-permute-start.22 = (f32[2,2560]{1,0:T(2,128)S(1)}, f32[2,2560]{1,0:T(2,128)S(1)}, u32[]{:S(2)}, u32[]{:S(2)}) collective-permute-start(f32[2,2560]{1,0:T(2,128)S(1)} %get-tuple-element.25), channel_id=1, source_target_pairs={{0,14},{1,15},{2,0},{3,1},{4,2},{5,3},{6,4},{7,5},{8,6},{9,7},{10,... | collective-permute-start | bytes 61448 | tf_op jit(solution)/shard_map/ppermute | solution.py:21
  184.1 3.9 %collective-permute-start.21 = (f32[2,2560]{1,0:T(2,128)S(1)}, f32[2,2560]{1,0:T(2,128)S(1)}, u32[]{:S(2)}, u32[]{:S(2)}) collective-permute-start(f32[2,2560]{1,0:T(2,128)S(1)} %get-tuple-element.26), channel_id=1, source_target_pairs={{0,64},{16,80},{32,96},{48,112},{64,128},{80,144},{96,160},{112,17... | collective-permute-start | bytes 61448 | tf_op jit(solution)/shard_map/ppermute | solution.py:21
  188.1 12.5 %collective-permute-done.21 = f32[2,2560]{1,0:T(2,128)S(1)} collective-permute-done((f32[2,2560]{1,0:T(2,128)S(1)}, f32[2,2560]{1,0:T(2,128)S(1)}, u32[]{:S(2)}, u32[]{:S(2)}) %collective-permute-start.21) | collective-permute-done | bytes 20512 | tf_op jit(solution)/shard_map/ppermute | solution.py:21
  200.6 3.1 %collective-permute-start.24 = (f32[4,2,2560]{2,1,0:T(2,128)S(1)}, f32[4,2,2560]{2,1,0:T(2,128)S(1)}, u32[]{:S(2)}, u32[]{:S(2)}) collective-permute-start(f32[4,2,2560]{2,1,0:T(2,128)S(1)} %maximum_add_fusion.1), channel_id=1, source_target_pairs={{0,16},{16,0},{32,48},{48,32},{64,80},{80,64},{96,112},{112,96},{1... | collective-permute-start | bytes 245768 | tf_op jit(solution)/shard_map/ppermute | solution.py:16
  203.7 4.0 %collective-permute-done.24 = f32[4,2,2560]{2,1,0:T(2,128)S(1)} collective-permute-done((f32[4,2,2560]{2,1,0:T(2,128)S(1)}, f32[4,2,2560]{2,1,0:T(2,128)S(1)}, u32[]{:S(2)}, u32[]{:S(2)}) %collective-permute-start.24) | collective-permute-done | bytes 81952 | tf_op jit(solution)/shard_map/ppermute | solution.py:16
  209.8 5.9 %collective-permute-done.25 = f32[4,2,2560]{2,1,0:T(2,128)S(1)} collective-permute-done((f32[4,2,2560]{2,1,0:T(2,128)S(1)}, f32[4,2,2560]{2,1,0:T(2,128)S(1)}, u32[]{:S(2)}, u32[]{:S(2)}) %collective-permute-start.25) | collective-permute-done | bytes 81952 | tf_op jit(solution)/shard_map/ppermute | solution.py:16
  215.7 5.7 %fusion = f32[320,2560]{1,0:T(8,128)} fusion(f32[320,2560]{1,0:T(8,128)} %copy-done.1, f32[4,2,2560]{2,1,0:T(2,128)S(1)} %fusion.61, f32[4,2,2560]{2,1,0:T(2,128)S(1)} %collective-permute-done.25, f32[4]{0:T(128)S(1)} %fusion.33, f32[4,1,320]{2,1,0:T(1,128)S(1)} %get-tuple-element.15, f32[4,1,320]{2,1,0:T(1,128)S(1)} %get-tuple-element.16), kind=kOutput, calls=%fused_computation.2 | convolution fusion | flops 79505920 | bytes 6727696 | tf_op jit(solution)/shard_map/fk,fm->km/dot_general | solution.py:140
  (82 shorter events, 51.7 us)
Async XLA Ops:
  6.0 32.3 %collective-permute-start.1 = (f32[2,320]{1,0:T(2,128)S(1)}, f32[2,320]{1,0:T(2,128)S(1)}, u32[]{:S(2)}, u32[]{:S(2)}) collective-permute-start(f32[2,320]{1,0:T(2,128)S(1)} %get-tuple-element.35), channel_id=1, source_target_pairs={{0,448},{16,464},{32,480},{48,496},{64,0},{80,16},{96,32},{112,48}... | collective-permute-start | bytes 7688 | tf_op jit(solution)/shard_map/ppermute | solution.py:21
  23.9 14.4 %collective-permute-start.4 = (f32[2,320]{1,0:T(2,128)S(1)}, f32[2,320]{1,0:T(2,128)S(1)}, u32[]{:S(2)}, u32[]{:S(2)}) collective-permute-start(f32[2,320]{1,0:T(2,128)S(1)} %get-tuple-element.36), channel_id=1, source_target_pairs={{0,2},{1,3},{2,4},{3,5},{4,6},{5,7},{6,8},{7,9},{8,10},{9,11},{10,... | collective-permute-start | bytes 7688 | tf_op jit(solution)/shard_map/ppermute | solution.py:21
  26.9 11.5 %collective-permute-start.3 = (f32[2,320]{1,0:T(2,128)S(1)}, f32[2,320]{1,0:T(2,128)S(1)}, u32[]{:S(2)}, u32[]{:S(2)}) collective-permute-start(f32[2,320]{1,0:T(2,128)S(1)} %get-tuple-element.37), channel_id=1, source_target_pairs={{0,14},{1,15},{2,0},{3,1},{4,2},{5,3},{6,4},{7,5},{8,6},{9,7},{10,... | collective-permute-start | bytes 7688 | tf_op jit(solution)/shard_map/ppermute | solution.py:21
  36.4 16.3 %collective-permute-start.2 = (f32[2,320]{1,0:T(2,128)S(1)}, f32[2,320]{1,0:T(2,128)S(1)}, u32[]{:S(2)}, u32[]{:S(2)}) collective-permute-start(f32[2,320]{1,0:T(2,128)S(1)} %get-tuple-element.38), channel_id=1, source_target_pairs={{0,64},{16,80},{32,96},{48,112},{64,128},{80,144},{96,160},{112,17... | collective-permute-start | bytes 7688 | tf_op jit(solution)/shard_map/ppermute | solution.py:21
  52.8 5.5 %collective-permute-start.5 = (f32[3,4]{1,0:T(4,128)S(1)}, f32[3,4]{1,0:T(4,128)S(1)}, u32[]{:S(2)}, u32[]{:S(2)}) collective-permute-start(f32[3,4]{1,0:T(4,128)S(1)} %pad_maximum_fusion.2), channel_id=1, source_target_pairs={{0,16},{16,0},{32,48},{48,32},{64,80},{80,64},{96,112},{112,96},{1... | collective-permute-start | bytes 152 | tf_op jit(solution)/shard_map/ppermute | solution.py:16
  58.3 7.0 %collective-permute-start.6 = (f32[3,4]{1,0:T(4,128)S(1)}, f32[3,4]{1,0:T(4,128)S(1)}, u32[]{:S(2)}, u32[]{:S(2)}) collective-permute-start(f32[3,4]{1,0:T(4,128)S(1)} %fusion.42), channel_id=1, source_target_pairs={{0,32},{16,48},{32,0},{48,16},{64,96},{80,112},{96,64},{112,80},{1... | collective-permute-start | bytes 152 | tf_op jit(solution)/shard_map/ppermute | solution.py:16
  66.3 18.4 %collective-permute-start.7 = (f32[2,2560]{1,0:T(2,128)S(1)}, f32[2,2560]{1,0:T(2,128)S(1)}, u32[]{:S(2)}, u32[]{:S(2)}) collective-permute-start(f32[2,2560]{1,0:T(2,128)S(1)} %get-tuple-element.27), channel_id=1, source_target_pairs={{0,448},{16,464},{32,480},{48,496},{64,0},{80,16},{96,32},{112,48}... | collective-permute-start | bytes 61448 | tf_op jit(solution)/shard_map/ppermute | solution.py:21
  68.2 16.5 %collective-permute-start.10 = (f32[2,2560]{1,0:T(2,128)S(1)}, f32[2,2560]{1,0:T(2,128)S(1)}, u32[]{:S(2)}, u32[]{:S(2)}) collective-permute-start(f32[2,2560]{1,0:T(2,128)S(1)} %get-tuple-element.28), channel_id=1, source_target_pairs={{0,2},{1,3},{2,4},{3,5},{4,6},{5,7},{6,8},{7,9},{8,10},{9,11},{10,... | collective-permute-start | bytes 61448 | tf_op jit(solution)/shard_map/ppermute | solution.py:21
  70.1 14.5 %collective-permute-start.9 = (f32[2,2560]{1,0:T(2,128)S(1)}, f32[2,2560]{1,0:T(2,128)S(1)}, u32[]{:S(2)}, u32[]{:S(2)}) collective-permute-start(f32[2,2560]{1,0:T(2,128)S(1)} %get-tuple-element.29), channel_id=1, source_target_pairs={{0,14},{1,15},{2,0},{3,1},{4,2},{5,3},{6,4},{7,5},{8,6},{9,7},{10,... | collective-permute-start | bytes 61448 | tf_op jit(solution)/shard_map/ppermute | solution.py:21
  80.7 16.5 %collective-permute-start.8 = (f32[2,2560]{1,0:T(2,128)S(1)}, f32[2,2560]{1,0:T(2,128)S(1)}, u32[]{:S(2)}, u32[]{:S(2)}) collective-permute-start(f32[2,2560]{1,0:T(2,128)S(1)} %get-tuple-element.30), channel_id=1, source_target_pairs={{0,64},{16,80},{32,96},{48,112},{64,128},{80,144},{96,160},{112,17... | collective-permute-start | bytes 61448 | tf_op jit(solution)/shard_map/ppermute | solution.py:21
  97.2 6.5 %collective-permute-start.11 = (f32[4,2,2560]{2,1,0:T(2,128)S(1)}, f32[4,2,2560]{2,1,0:T(2,128)S(1)}, u32[]{:S(2)}, u32[]{:S(2)}) collective-permute-start(f32[4,2,2560]{2,1,0:T(2,128)S(1)} %maximum_add_fusion), channel_id=1, source_target_pairs={{0,16},{16,0},{32,48},{48,32},{64,80},{80,64},{96,112},{112,96},{1... | collective-permute-start | bytes 245768 | tf_op jit(solution)/shard_map/ppermute | solution.py:16
  103.8 7.8 %collective-permute-start.12 = (f32[4,2,2560]{2,1,0:T(2,128)S(1)}, f32[4,2,2560]{2,1,0:T(2,128)S(1)}, u32[]{:S(2)}, u32[]{:S(2)}) collective-permute-start(f32[4,2,2560]{2,1,0:T(2,128)S(1)} %fusion.63), channel_id=1, source_target_pairs={{0,32},{16,48},{32,0},{48,16},{64,96},{80,112},{96,64},{112,80},{1... | collective-permute-start | bytes 245768 | tf_op jit(solution)/shard_map/ppermute | solution.py:16
  121.8 18.3 %collective-permute-start.14 = (f32[2,320]{1,0:T(2,128)S(1)}, f32[2,320]{1,0:T(2,128)S(1)}, u32[]{:S(2)}, u32[]{:S(2)}) collective-permute-start(f32[2,320]{1,0:T(2,128)S(1)} %get-tuple-element.31), channel_id=1, source_target_pairs={{0,448},{16,464},{32,480},{48,496},{64,0},{80,16},{96,32},{112,48}... | collective-permute-start | bytes 7688 | tf_op jit(solution)/shard_map/ppermute | solution.py:21
  123.7 16.4 %collective-permute-start.17 = (f32[2,320]{1,0:T(2,128)S(1)}, f32[2,320]{1,0:T(2,128)S(1)}, u32[]{:S(2)}, u32[]{:S(2)}) collective-permute-start(f32[2,320]{1,0:T(2,128)S(1)} %get-tuple-element.32), channel_id=1, source_target_pairs={{0,2},{1,3},{2,4},{3,5},{4,6},{5,7},{6,8},{7,9},{8,10},{9,11},{10,... | collective-permute-start | bytes 7688 | tf_op jit(solution)/shard_map/ppermute | solution.py:21
  125.7 14.5 %collective-permute-start.16 = (f32[2,320]{1,0:T(2,128)S(1)}, f32[2,320]{1,0:T(2,128)S(1)}, u32[]{:S(2)}, u32[]{:S(2)}) collective-permute-start(f32[2,320]{1,0:T(2,128)S(1)} %get-tuple-element.33), channel_id=1, source_target_pairs={{0,14},{1,15},{2,0},{3,1},{4,2},{5,3},{6,4},{7,5},{8,6},{9,7},{10,... | collective-permute-start | bytes 7688 | tf_op jit(solution)/shard_map/ppermute | solution.py:21
  136.2 16.3 %collective-permute-start.15 = (f32[2,320]{1,0:T(2,128)S(1)}, f32[2,320]{1,0:T(2,128)S(1)}, u32[]{:S(2)}, u32[]{:S(2)}) collective-permute-start(f32[2,320]{1,0:T(2,128)S(1)} %get-tuple-element.34), channel_id=1, source_target_pairs={{0,64},{16,80},{32,96},{48,112},{64,128},{80,144},{96,160},{112,17... | collective-permute-start | bytes 7688 | tf_op jit(solution)/shard_map/ppermute | solution.py:21
  152.7 5.5 %collective-permute-start.18 = (f32[3,4]{1,0:T(4,128)S(1)}, f32[3,4]{1,0:T(4,128)S(1)}, u32[]{:S(2)}, u32[]{:S(2)}) collective-permute-start(f32[3,4]{1,0:T(4,128)S(1)} %pad_maximum_fusion.3), channel_id=1, source_target_pairs={{0,16},{16,0},{32,48},{48,32},{64,80},{80,64},{96,112},{112,96},{1... | collective-permute-start | bytes 152 | tf_op jit(solution)/shard_map/ppermute | solution.py:16
  158.2 7.0 %collective-permute-start.19 = (f32[3,4]{1,0:T(4,128)S(1)}, f32[3,4]{1,0:T(4,128)S(1)}, u32[]{:S(2)}, u32[]{:S(2)}) collective-permute-start(f32[3,4]{1,0:T(4,128)S(1)} %fusion.41), channel_id=1, source_target_pairs={{0,32},{16,48},{32,0},{48,16},{64,96},{80,112},{96,64},{112,80},{1... | collective-permute-start | bytes 152 | tf_op jit(solution)/shard_map/ppermute | solution.py:16
  169.7 18.4 %collective-permute-start.20 = (f32[2,2560]{1,0:T(2,128)S(1)}, f32[2,2560]{1,0:T(2,128)S(1)}, u32[]{:S(2)}, u32[]{:S(2)}) collective-permute-start(f32[2,2560]{1,0:T(2,128)S(1)} %get-tuple-element.23), channel_id=1, source_target_pairs={{0,448},{16,464},{32,480},{48,496},{64,0},{80,16},{96,32},{112,48}... | collective-permute-start | bytes 61448 | tf_op jit(solution)/shard_map/ppermute | solution.py:21
  171.6 16.5 %collective-permute-start.23 = (f32[2,2560]{1,0:T(2,128)S(1)}, f32[2,2560]{1,0:T(2,128)S(1)}, u32[]{:S(2)}, u32[]{:S(2)}) collective-permute-start(f32[2,2560]{1,0:T(2,128)S(1)} %get-tuple-element.24), channel_id=1, source_target_pairs={{0,2},{1,3},{2,4},{3,5},{4,6},{5,7},{6,8},{7,9},{8,10},{9,11},{10,... | collective-permute-start | bytes 61448 | tf_op jit(solution)/shard_map/ppermute | solution.py:21
  173.5 14.5 %collective-permute-start.22 = (f32[2,2560]{1,0:T(2,128)S(1)}, f32[2,2560]{1,0:T(2,128)S(1)}, u32[]{:S(2)}, u32[]{:S(2)}) collective-permute-start(f32[2,2560]{1,0:T(2,128)S(1)} %get-tuple-element.25), channel_id=1, source_target_pairs={{0,14},{1,15},{2,0},{3,1},{4,2},{5,3},{6,4},{7,5},{8,6},{9,7},{10,... | collective-permute-start | bytes 61448 | tf_op jit(solution)/shard_map/ppermute | solution.py:21
  184.1 16.5 %collective-permute-start.21 = (f32[2,2560]{1,0:T(2,128)S(1)}, f32[2,2560]{1,0:T(2,128)S(1)}, u32[]{:S(2)}, u32[]{:S(2)}) collective-permute-start(f32[2,2560]{1,0:T(2,128)S(1)} %get-tuple-element.26), channel_id=1, source_target_pairs={{0,64},{16,80},{32,96},{48,112},{64,128},{80,144},{96,160},{112,17... | collective-permute-start | bytes 61448 | tf_op jit(solution)/shard_map/ppermute | solution.py:21
  200.6 7.1 %collective-permute-start.24 = (f32[4,2,2560]{2,1,0:T(2,128)S(1)}, f32[4,2,2560]{2,1,0:T(2,128)S(1)}, u32[]{:S(2)}, u32[]{:S(2)}) collective-permute-start(f32[4,2,2560]{2,1,0:T(2,128)S(1)} %maximum_add_fusion.1), channel_id=1, source_target_pairs={{0,16},{16,0},{32,48},{48,32},{64,80},{80,64},{96,112},{112,96},{1... | collective-permute-start | bytes 245768 | tf_op jit(solution)/shard_map/ppermute | solution.py:16
  207.8 7.8 %collective-permute-start.25 = (f32[4,2,2560]{2,1,0:T(2,128)S(1)}, f32[4,2,2560]{2,1,0:T(2,128)S(1)}, u32[]{:S(2)}, u32[]{:S(2)}) collective-permute-start(f32[4,2,2560]{2,1,0:T(2,128)S(1)} %fusion.61), channel_id=1, source_target_pairs={{0,32},{16,48},{32,0},{48,16},{64,96},{80,112},{96,64},{112,80},{1... | collective-permute-start | bytes 245768 | tf_op jit(solution)/shard_map/ppermute | solution.py:16
  (4 other events, 10.4 us)
where the time goes:
time: 222 us; the launch traced here: 221 us
  starting transfers between devices  112 us (50%)
  waiting for transfers between devices  82.5 us (37%)
  matrix products  19.1 us (9%)
  other arithmetic  3.63 us (2%)
  local copies, waits for them, and re-layouts  3.2 us (1%)
    ppermute x16, starting transfers between devices, from_behind(): lax.ppermute(value, axis, [(i, (i + by) % length) for i in range(length)])  87.2 us
    ppermute x16, waiting for transfers between devices, from_behind(): lax.ppermute(value, axis, [(i, (i + by) % length) for i in range(length)])  51.7 us
    ppermute x10, waiting for transfers between devices, swapped(): lax.ppermute(value, axis, [(i, i ^ 1 << apart) for i in range(lax.axis_si...  30.9 us
    ppermute x10, starting transfers between devices, swapped(): lax.ppermute(value, axis, [(i, i ^ 1 << apart) for i in range(lax.axis_si...  25.3 us
    dot_general x2, matrix products, per_device(): jnp.einsum('fk,fm->km', flat_directions, weighted, precision=highest)  8.53 us
  transfers between devices with their start and end apart: 26, of which 14 were waited for; matrix products, arithmetic and copies ran while one was open for 2% of the time, Pallas kernels for 0%

commit v1 on v0

v1 whole, which is shorter than its diff:
```python
import functools

import jax
import jax.numpy as jnp
from jax import lax
from jax.experimental import pallas as pl
from jax.experimental.pallas import tpu as pltpu
from jax.sharding import PartitionSpec as P

ROUNDS = 2
ROW_SHARDS = 4
COL_SHARDS = 2
SLOTS = 4
RANK = 2
EDGE_ROWS = SLOTS * RANK
PRIME = 8191
EPSILON = 1e-06
MESH_ID = pl.DeviceIdType.MESH
NT = (((1,), (1,)), ((), ()))
NN = (((1,), (0,)), ((), ()))
TN = (((0,), (0,)), ((), ()))


def product(left, right, dims):
    return lax.dot_general(left, right, dims, preferred_element_type=jnp.float32)


def halves(values):
    high = values.astype(jnp.bfloat16)
    return high, (values - high.astype(jnp.float32)).astype(jnp.bfloat16)


def stacked_halves(values):
    return jnp.concatenate(halves(values), axis=0)


def folded(values):
    return (values & PRIME) + (values >> 13)


def start_factors(seed_column, first_column, width):
    column = first_column + lax.broadcasted_iota(jnp.int32, (EDGE_ROWS, width), 1)
    square = folded(column * column)
    residue = folded(folded(square * (seed_column + 1) + column * 17))
    residue = jnp.where(residue >= PRIME, residue - PRIME, residue)
    return residue.astype(jnp.float32) * (2.0 / 8191.0) - 1.0


def column_of(scalars):
    row = lax.broadcasted_iota(jnp.int32, (EDGE_ROWS, 1), 0)
    values = jnp.full((EDGE_ROWS, 1), scalars[0])
    for index in range(1, EDGE_ROWS):
        values = jnp.where(row == index, scalars[index], values)
    return values


def partner_rows(values):
    row = lax.broadcasted_iota(jnp.int32, values.shape, 0)
    down = pltpu.roll(values, 1, 0)
    up = pltpu.roll(values, EDGE_ROWS - 1, 0)
    return jnp.where(row % 2 == 0, up, down)


def gram(directions):
    norm = jnp.sum(directions * directions, axis=1, keepdims=True)
    cross = jnp.sum(directions * partner_rows(directions), axis=1, keepdims=True)
    lane = lax.broadcasted_iota(jnp.int32, (EDGE_ROWS, 128), 1)
    return jnp.where(lane == 0, norm, jnp.where(lane == 1, cross, 0.0))


def normalizers(statistics):
    row = lax.broadcasted_iota(jnp.int32, (EDGE_ROWS, 128), 0)
    norm = jnp.broadcast_to(statistics[:, 0:1], (EDGE_ROWS, 128))
    cross = jnp.broadcast_to(statistics[:, 1:2], (EDGE_ROWS, 128))
    other = partner_rows(norm)
    first = row % 2 == 0
    lead = jnp.where(first, norm, other)
    rest = jnp.where(first, other, norm)
    share = jnp.where(cross == lead + EPSILON, 1.0, cross / (lead + EPSILON))
    left_over = (rest - share * cross) - share * (cross - share * lead)
    left_over = jnp.maximum(left_over, 0.0)
    scale = 1.0 / jnp.sqrt(jnp.where(first, lead, left_over) + EPSILON)
    share = jnp.where(first, 0.0, share)
    return scale[:, 0:1], share[:, 0:1]


def normalized(values, scale, share):
    return (values - share * partner_rows(values)) * scale


def rows_of(slabs):
    return jnp.concatenate([slabs[slot] for slot in range(SLOTS)], axis=0)


def consensus(
    x_hbm, seeds, counts, left_out, right_out, x, images, image_pair, image_near,
    stats, parts, parts_in, sums, sums_in, shares, x_sem, image_send, image_recv,
    stat_send, stat_recv, part_send, part_recv, sum_send, sum_recv, share_send, share_recv,
):
    local_rows, width = x.shape
    quarter = width // ROW_SHARDS
    graph_rows, graph_cols = seeds.shape[0], seeds.shape[1]
    row, col = lax.axis_index("row"), lax.axis_index("col")
    node_row, shard = row // ROW_SHARDS, row % ROW_SHARDS
    node_col, core = col // COL_SHARDS, col % COL_SHARDS
    below = (node_row + 1) % graph_rows
    above = (node_row + graph_rows - 1) % graph_rows
    right = (node_col + 1) % graph_cols
    left = (node_col + graph_cols - 1) % graph_cols
    neighbours = [(below, node_col), (above, node_col), (node_row, right), (node_row, left)]

    def device(node, at_shard, at_core):
        return (node[0] * ROW_SHARDS + at_shard, node[1] * COL_SHARDS + at_core)

    sibling = device((node_row, node_col), shard, 1 - core)
    shard_peers = [
        device((node_row, node_col), (shard + apart) % ROW_SHARDS, core)
        for apart in range(1, ROW_SHARDS)
    ]

    load = pltpu.make_async_copy(x_hbm, x, x_sem)
    load.start()
    barrier = pltpu.get_barrier_semaphore()
    partners = [device(node, shard, at) for node in neighbours for at in range(COL_SHARDS)]
    partners += [sibling] + shard_peers
    for partner in partners:
        pl.semaphore_signal(barrier, inc=1, device_id=partner, device_id_type=MESH_ID)

    owners = [(node_row, node_col, 0), (above, node_col, 0), (node_row, node_col, 1), (node_row, left, 1)]
    seed_column = column_of([seeds[r, c, a, k] for r, c, a in owners for k in range(RANK)])
    weight = column_of([counts[r, c, a] for r, c, a in owners for _ in range(RANK)])
    weight = weight.astype(jnp.float32) * (-1.0 / 16.0)
    factors = start_factors(seed_column, core * width, width)

    sent = []

    def send(source, target, send_sem, recv_sem, to):
        copy = pltpu.make_async_remote_copy(
            src_ref=source, dst_ref=target, send_sem=send_sem, recv_sem=recv_sem,
            device_id=to, device_id_type=MESH_ID,
        )
        copy.start()
        sent.append(copy)
        return copy

    lefts, rights = [], []
    load.wait()
    for turn in range(ROUNDS):
        factor_halves = stacked_halves(factors)
        image = product(factor_halves, x[...], NT)
        image = image[:EDGE_ROWS] + image[EDGE_ROWS:]
        if turn > 0:
            overlap = product(factor_halves, factor_halves, NT)
            overlap = overlap[:EDGE_ROWS] + overlap[EDGE_ROWS:]
            overlap = overlap[:, :EDGE_ROWS] + overlap[:, EDGE_ROWS:]
            weighted = weight * lefts[0]
            for g in range(EDGE_ROWS):
                image = image + overlap[:, g : g + 1] * weighted[g : g + 1, :]
        for slot in range(SLOTS):
            images[turn, slot] = image[RANK * slot : RANK * (slot + 1), :]
        if turn == 0:
            pl.semaphore_wait(barrier, len(partners))
        arrivals = []
        for slot, node in enumerate(neighbours):
            for at in range(COL_SHARDS):
                arrivals.append(
                    send(
                        images.at[turn, slot], image_near.at[turn, slot ^ 1, core],
                        image_send.at[turn, slot, at], image_recv.at[turn, slot ^ 1, core],
                        device(node, shard, at),
                    )
                )
        pair = send(images.at[turn], image_pair.at[turn], image_send.at[turn, SLOTS, 0], image_recv.at[turn, SLOTS, 0], sibling)
        pair.wait_recv()
        own = image + rows_of([image_pair[turn, slot] for slot in range(SLOTS)])
        for slot in range(SLOTS):
            for at in range(COL_SHARDS):
                pltpu.make_async_remote_copy(
                    src_ref=images.at[turn, slot], dst_ref=image_near.at[turn, slot, at],
                    send_sem=image_send.at[turn, slot, at], recv_sem=image_recv.at[turn, slot, at],
                    device_id=sibling, device_id_type=MESH_ID,
                ).wait_recv()
        near = rows_of([image_near[turn, slot, 0] + image_near[turn, slot, 1] for slot in range(SLOTS)])
        directions = own - near

        stats[turn, shard] = gram(directions)
        stat_copies = [
            send(
                stats.at[turn, shard], stats.at[turn, shard],
                stat_send.at[turn, apart], stat_recv.at[turn, apart], peer,
            )
            for apart, peer in enumerate(shard_peers)
        ]
        direction_halves = stacked_halves(directions)
        projection = product(direction_halves, x[...], NN)
        projection = projection[:EDGE_ROWS] + projection[EDGE_ROWS:]
        if turn > 0:
            overlap = product(direction_halves, stacked_halves(lefts[0]), NT)
            overlap = overlap[:EDGE_ROWS] + overlap[EDGE_ROWS:]
            overlap = overlap[:, :EDGE_ROWS] + overlap[:, EDGE_ROWS:]
            for g in range(EDGE_ROWS):
                projection = projection + overlap[:, g : g + 1] * rights[0][g : g + 1, :]
        for part in range(ROW_SHARDS):
            parts[turn, part] = projection[:, part * quarter : (part + 1) * quarter]
        part_copies = []
        for apart, peer in enumerate(shard_peers):
            part_copies.append(
                send(
                    parts.at[turn, (shard + apart + 1) % ROW_SHARDS], parts_in.at[turn, apart],
                    part_send.at[turn, apart], part_recv.at[turn, apart], peer,
                )
            )
        for copy in part_copies:
            copy.wait_recv()
        total = parts[turn, shard]
        for apart in range(ROW_SHARDS - 1):
            total = total + parts_in[turn, apart]
        for slot in range(SLOTS):
            sums[turn, slot] = total[RANK * slot : RANK * (slot + 1), :]
        sum_copies = []
        for slot, node in enumerate(neighbours):
            sum_copies.append(
                send(
                    sums.at[turn, slot], sums_in.at[turn, slot ^ 1],
                    sum_send.at[turn, slot], sum_recv.at[turn, slot ^ 1],
                    device(node, shard, core),
                )
            )
        for copy in stat_copies:
            copy.wait_recv()
        statistics = (stats[turn, 0] + stats[turn, 1]) + (stats[turn, 2] + stats[turn, 3])
        scale, share = normalizers(statistics)
        lefts.append(normalized(directions, scale, share))
        for copy in sum_copies:
            copy.wait_recv()
        total = total + rows_of([sums_in[turn, slot] for slot in range(SLOTS)])
        shares[turn, shard] = normalized(total, scale, share)
        share_copies = [
            send(
                shares.at[turn, shard], shares.at[turn, shard],
                share_send.at[turn, apart], share_recv.at[turn, apart], peer,
            )
            for apart, peer in enumerate(shard_peers)
        ]
        if turn == ROUNDS - 1:
            left_out[...] = jnp.concatenate(lefts, axis=0)
        for copy in share_copies:
            copy.wait_recv()
        factors = jnp.concatenate([shares[turn, part] for part in range(ROW_SHARDS)], axis=1)
        rights.append(weight * factors)
    right_out[...] = jnp.concatenate(rights, axis=0)
    for copy in sent:
        copy.wait_send()


def outer(left_ref, right_ref, out_hbm, block, sem):
    left_high, left_low = halves(left_ref[...])
    left = jnp.concatenate([left_high, left_high, left_low], axis=0)
    chunk = block.shape[2]
    copies = []
    for step in range(block.shape[0]):
        at = pl.ds(step * chunk, chunk)
        right_high, right_low = halves(right_ref[:, at])
        right = jnp.concatenate([right_high, right_low, right_high], axis=0)
        block[step] = product(left, right, TN)
        copy = pltpu.make_async_copy(block.at[step], out_hbm.at[:, at], sem.at[step])
        copy.start()
        copies.append(copy)
    for copy in copies:
        copy.wait()


def per_device(replicas, factor_seeds, edge_counts):
    rows, width = replicas.shape
    quarter = width // ROW_SHARDS
    both = ROUNDS * EDGE_ROWS
    peers = ROW_SHARDS - 1
    f32 = jnp.float32
    dma = pltpu.SemaphoreType.DMA
    left, right = pl.pallas_call(
        consensus,
        out_shape=[
            jax.ShapeDtypeStruct((both, rows), f32),
            jax.ShapeDtypeStruct((both, width), f32),
        ],
        in_specs=[
            pl.BlockSpec(memory_space=pl.ANY),
            pl.BlockSpec(memory_space=pltpu.SMEM),
            pl.BlockSpec(memory_space=pltpu.SMEM),
        ],
        out_specs=[pl.BlockSpec(memory_space=pltpu.VMEM)] * 2,
        scratch_shapes=[
            pltpu.VMEM((rows, width), replicas.dtype),
            pltpu.VMEM((ROUNDS, SLOTS, RANK, rows), f32),
            pltpu.VMEM((ROUNDS, SLOTS, RANK, rows), f32),
            pltpu.VMEM((ROUNDS, SLOTS, COL_SHARDS, RANK, rows), f32),
            pltpu.VMEM((ROUNDS, ROW_SHARDS, EDGE_ROWS, 128), f32),
            pltpu.VMEM((ROUNDS, ROW_SHARDS, EDGE_ROWS, quarter), f32),
            pltpu.VMEM((ROUNDS, peers, EDGE_ROWS, quarter), f32),
            pltpu.VMEM((ROUNDS, SLOTS, RANK, quarter), f32),
            pltpu.VMEM((ROUNDS, SLOTS, RANK, quarter), f32),
            pltpu.VMEM((ROUNDS, ROW_SHARDS, EDGE_ROWS, quarter), f32),
            dma,
            dma((ROUNDS, SLOTS + 1, COL_SHARDS)),
            dma((ROUNDS, SLOTS + 1, COL_SHARDS)),
            dma((ROUNDS, peers)),
            dma((ROUNDS, peers)),
            dma((ROUNDS, peers)),
            dma((ROUNDS, peers)),
            dma((ROUNDS, SLOTS)),
            dma((ROUNDS, SLOTS)),
            dma((ROUNDS, peers)),
            dma((ROUNDS, peers)),
        ],
        compiler_params=pltpu.CompilerParams(collective_id=0, has_side_effects=True),
        name="consensus",
    )(replicas, factor_seeds, edge_counts)
    chunks = 5
    return pl.pallas_call(
        outer,
        out_shape=jax.ShapeDtypeStruct((rows, width), f32),
        in_specs=[pl.BlockSpec(memory_space=pltpu.VMEM)] * 2,
        out_specs=pl.BlockSpec(memory_space=pl.ANY),
        scratch_shapes=[pltpu.VMEM((chunks, rows, width // chunks), f32), dma((chunks,))],
        name="outer",
    )(left, right)


def solution(mesh):
    return jax.shard_map(
        per_device,
        mesh=mesh,
        in_specs=(P("row", "col"), P(), P()),
        out_specs=P("row", "col"),
        check_vma=False,
    )
```

time: 222 us -> 76.1 us (0.34)
  the two profiles are of different devices: /device:TPU:16 before, /device:TPU:1 now
where the time goes in v1:
time: 76.1 us; the launch traced here: 75.2 us
  Pallas kernels  72.3 us (95%)
  local copies, waits for them, and re-layouts  2.93 us (4%)
    pallas_call x1, Pallas kernels, per_device(): pl.pallas_call(consensus, out_shape=[jax.ShapeDtypeStruct((both, rows), f...  69.3 us
    pallas_call x1, Pallas kernels, per_device(): pl.pallas_call(outer, out_shape=jax.ShapeDtypeStruct((rows, width), f32),...  2.94 us
    unnamed x2, local copies, waits for them, and re-layouts  2.93 us

profile of v1, /device:TPU:1, one launch (start us, length us, event | category | flops | bytes accessed | tf_op | source)
XLA Modules:
  0.0 75.2 jit_solution(6941131103782272967)
XLA Ops:
  0.0 1.4 %copy.5.counts = s32[8,8,2]{2,1,0:T(8,128)} copy(s32[8,8,2]{1,2,0:T(2,128)} %param.5) | data formatting | bytes 1024 | tf_op args[2]
  1.4 1.5 %copy.4.seeds = s32[8,8,2,2]{3,2,1,0:T(2,128)} copy(s32[8,8,2,2]{1,3,2,0:T(2,128)} %param.4) | data formatting | bytes 2048 | tf_op args[1]
  2.9 69.3 %consensus.1 = (f32[16,320]{1,0:T(8,128)}, f32[16,2560]{1,0:T(8,128)}) custom-call(bf16[320,2560]{1,0:T(8,128)(2,1)} %x_hbm.1, s32[8,8,2,2]{3,2,1,0:T(2,128)} %copy.4.seeds, s32[8,8,2]{2,1,0:T(8,128)} %copy.5.counts), custom_call_target="tpu_custom_call" | custom-call | tf_op jit(solution)/shard_map/consensus/pallas_call | solution.py:280
  72.3 2.9 %outer.1 = f32[320,2560]{1,0:T(8,128)} custom-call(f32[16,320]{1,0:T(8,128)} %get-tuple-element.7.left_ref, f32[16,2560]{1,0:T(8,128)} %get-tuple-element.8.right_ref), custom_call_target="tpu_custom_call" | custom-call | tf_op jit(solution)/shard_map/outer/pallas_call | solution.py:319

commit v2 on v1

--- a/solution.py
+++ b/solution.py
@@ -15,6 +15,8 @@
 EDGE_ROWS = SLOTS * RANK
 PRIME = 8191
 EPSILON = 1e-06
+VMEM_BYTES = 12 << 20
+PART_ORDER = (2, 1, 3, 0)
 MESH_ID = pl.DeviceIdType.MESH
 NT = (((1,), (1,)), ((), ()))
 NN = (((1,), (0,)), ((), ()))
@@ -93,13 +95,13 @@
 
 
 def consensus(
-    x_hbm, seeds, counts, left_out, right_out, x, images, image_pair, image_near,
-    stats, parts, parts_in, sums, sums_in, shares, x_sem, image_send, image_recv,
+    x_hbm, seeds_hbm, counts_hbm, left_out, right_out, x, seeds, counts, images, image_pair, image_near,
+    stats, parts, parts_in, sums, sums_in, shares, load_sem, image_send, image_recv,
     stat_send, stat_recv, part_send, part_recv, sum_send, sum_recv, share_send, share_recv,
 ):
-    local_rows, width = x.shape
-    quarter = width // ROW_SHARDS
-    graph_rows, graph_cols = seeds.shape[0], seeds.shape[1]
+    quarter = x.shape[2]
+    width = ROW_SHARDS * quarter
+    graph_rows, graph_cols = seeds.shape[0], seeds.shape[3]
     row, col = lax.axis_index("row"), lax.axis_index("col")
     node_row, shard = row // ROW_SHARDS, row % ROW_SHARDS
     node_col, core = col // COL_SHARDS, col % COL_SHARDS
@@ -118,17 +120,25 @@
         for apart in range(1, ROW_SHARDS)
     ]
 
-    load = pltpu.make_async_copy(x_hbm, x, x_sem)
-    load.start()
     barrier = pltpu.get_barrier_semaphore()
     partners = [device(node, shard, at) for node in neighbours for at in range(COL_SHARDS)]
     partners += [sibling] + shard_peers
     for partner in partners:
         pl.semaphore_signal(barrier, inc=1, device_id=partner, device_id_type=MESH_ID)
-
+    sources = [seeds_hbm, counts_hbm] + [x_hbm.at[:, pl.ds(part * quarter, quarter)] for part in range(ROW_SHARDS)]
+    targets = [seeds, counts] + [x.at[part] for part in range(ROW_SHARDS)]
+    loads = [
+        pltpu.make_async_copy(source, target, load_sem.at[index])
+        for index, (source, target) in enumerate(zip(sources, targets))
+    ]
+    for load in loads:
+        load.start()
+
+    loads[0].wait()
+    loads[1].wait()
     owners = [(node_row, node_col, 0), (above, node_col, 0), (node_row, node_col, 1), (node_row, left, 1)]
-    seed_column = column_of([seeds[r, c, a, k] for r, c, a in owners for k in range(RANK)])
-    weight = column_of([counts[r, c, a] for r, c, a in owners for _ in range(RANK)])
+    seed_column = column_of([seeds[r, a, k, c] for r, c, a in owners for k in range(RANK)])
+    weight = column_of([counts[r, a, c] for r, c, a in owners for _ in range(RANK)])
     weight = weight.astype(jnp.float32) * (-1.0 / 16.0)
     factors = start_factors(seed_column, core * width, width)
 
@@ -143,14 +153,29 @@
         sent.append(copy)
         return copy
 
-    lefts, rights = [], []
-    load.wait()
+    lefts = []
+    share_copies = None
     for turn in range(ROUNDS):
-        factor_halves = stacked_halves(factors)
-        image = product(factor_halves, x[...], NT)
+        image = None
+        overlap = None
+        for step in range(ROW_SHARDS):
+            if turn == 0:
+                part = step
+                loads[2 + part].wait()
+                factor = factors[:, part * quarter : (part + 1) * quarter]
+            else:
+                part = (shard + ROW_SHARDS - step) % ROW_SHARDS
+                if step > 0:
+                    share_copies[step - 1].wait_recv()
+                factor = shares[turn - 1, part]
+            factor_halves = stacked_halves(factor)
+            term = product(factor_halves, x[part], NT)
+            image = term if image is None else image + term
+            if turn > 0:
+                term = product(factor_halves, factor_halves, NT)
+                overlap = term if overlap is None else overlap + term
         image = image[:EDGE_ROWS] + image[EDGE_ROWS:]
         if turn > 0:
-            overlap = product(factor_halves, factor_halves, NT)
             overlap = overlap[:EDGE_ROWS] + overlap[EDGE_ROWS:]
             overlap = overlap[:, :EDGE_ROWS] + overlap[:, EDGE_ROWS:]
             weighted = weight * lefts[0]
@@ -183,6 +208,28 @@
         near = rows_of([image_near[turn, slot, 0] + image_near[turn, slot, 1] for slot in range(SLOTS)])
         directions = own - near
 
+        direction_halves = stacked_halves(directions)
+        if turn > 0:
+            overlap = product(direction_halves, stacked_halves(lefts[0]), NT)
+            overlap = overlap[:EDGE_ROWS] + overlap[EDGE_ROWS:]
+            overlap = overlap[:, :EDGE_ROWS] + overlap[:, EDGE_ROWS:]
+        part_copies = []
+        for apart in PART_ORDER:
+            part = (shard + apart) % ROW_SHARDS
+            projection = product(direction_halves, x[part], NN)
+            projection = projection[:EDGE_ROWS] + projection[EDGE_ROWS:]
+            if turn > 0:
+                weighted = weight * shares[0, part]
+                for g in range(EDGE_ROWS):
+                    projection = projection + overlap[:, g : g + 1] * weighted[g : g + 1, :]
+            parts[turn, part] = projection
+            if apart > 0:
+                part_copies.append(
+                    send(
+                        parts.at[turn, part], parts_in.at[turn, apart - 1],
+                        part_send.at[turn, apart - 1], part_recv.at[turn, apart - 1], shard_peers[apart - 1],
+                    )
+                )
         stats[turn, shard] = gram(directions)
         stat_copies = [
             send(
@@ -191,25 +238,6 @@
             )
             for apart, peer in enumerate(shard_peers)
         ]
-        direction_halves = stacked_halves(directions)
-        projection = product(direction_halves, x[...], NN)
-        projection = projection[:EDGE_ROWS] + projection[EDGE_ROWS:]
-        if turn > 0:
-            overlap = product(direction_halves, stacked_halves(lefts[0]), NT)
-            overlap = overlap[:EDGE_ROWS] + overlap[EDGE_ROWS:]
-            overlap = overlap[:, :EDGE_ROWS] + overlap[:, EDGE_ROWS:]
-            for g in range(EDGE_ROWS):
-                projection = projection + overlap[:, g : g + 1] * rights[0][g : g + 1, :]
-        for part in range(ROW_SHARDS):
-            parts[turn, part] = projection[:, part * quarter : (part + 1) * quarter]
-        part_copies = []
-        for apart, peer in enumerate(shard_peers):
-            part_copies.append(
-                send(
-                    parts.at[turn, (shard + apart + 1) % ROW_SHARDS], parts_in.at[turn, apart],
-                    part_send.at[turn, apart], part_recv.at[turn, apart], peer,
-                )
-            )
         for copy in part_copies:
             copy.wait_recv()
         total = parts[turn, shard]
@@ -242,13 +270,13 @@
             )
             for apart, peer in enumerate(shard_peers)
         ]
-        if turn == ROUNDS - 1:
-            left_out[...] = jnp.concatenate(lefts, axis=0)
-        for copy in share_copies:
-            copy.wait_recv()
-        factors = jnp.concatenate([shares[turn, part] for part in range(ROW_SHARDS)], axis=1)
-        rights.append(weight * factors)
-    right_out[...] = jnp.concatenate(rights, axis=0)
+    left_out[...] = jnp.concatenate(lefts, axis=0)
+    for copy in share_copies:
+        copy.wait_recv()
+    for turn in range(ROUNDS):
+        for part in range(ROW_SHARDS):
+            at = slice(part * quarter, (part + 1) * quarter)
+            right_out[turn * EDGE_ROWS : (turn + 1) * EDGE_ROWS, at] = weight * shares[turn, part]
     for copy in sent:
         copy.wait_send()
 
@@ -277,6 +305,8 @@
     peers = ROW_SHARDS - 1
     f32 = jnp.float32
     dma = pltpu.SemaphoreType.DMA
+    factor_seeds = factor_seeds.transpose(0, 2, 3, 1)
+    edge_counts = edge_counts.transpose(0, 2, 1)
     left, right = pl.pallas_call(
         consensus,
         out_shape=[
@@ -284,13 +314,15 @@
             jax.ShapeDtypeStruct((both, width), f32),
         ],
         in_specs=[
-            pl.BlockSpec(memory_space=pl.ANY),
-            pl.BlockSpec(memory_space=pltpu.SMEM),
-            pl.BlockSpec(memory_space=pltpu.SMEM),
+            pl.BlockSpec(memory_space=pltpu.HBM),
+            pl.BlockSpec(memory_space=pltpu.HBM),
+            pl.BlockSpec(memory_space=pltpu.HBM),
         ],
         out_specs=[pl.BlockSpec(memory_space=pltpu.VMEM)] * 2,
         scratch_shapes=[
-            pltpu.VMEM((rows, width), replicas.dtype),
+            pltpu.VMEM((ROW_SHARDS, rows, quarter), replicas.dtype),
+            pltpu.SMEM(factor_seeds.shape, jnp.int32),
+            pltpu.SMEM(edge_counts.shape, jnp.int32),
             pltpu.VMEM((ROUNDS, SLOTS, RANK, rows), f32),
             pltpu.VMEM((ROUNDS, SLOTS, RANK, rows), f32),
             pltpu.VMEM((ROUNDS, SLOTS, COL_SHARDS, RANK, rows), f32),
@@ -300,7 +332,7 @@
             pltpu.VMEM((ROUNDS, SLOTS, RANK, quarter), f32),
             pltpu.VMEM((ROUNDS, SLOTS, RANK, quarter), f32),
             pltpu.VMEM((ROUNDS, ROW_SHARDS, EDGE_ROWS, quarter), f32),
-            dma,
+            dma((2 + ROW_SHARDS,)),
             dma((ROUNDS, SLOTS + 1, COL_SHARDS)),
             dma((ROUNDS, SLOTS + 1, COL_SHARDS)),
             dma((ROUNDS, peers)),
@@ -312,9 +344,9 @@
             dma((ROUNDS, peers)),
             dma((ROUNDS, peers)),
         ],
-        compiler_params=pltpu.CompilerParams(collective_id=0, has_side_effects=True),
+        compiler_params=pltpu.CompilerParams(collective_id=0, has_side_effects=True, vmem_limit_bytes=VMEM_BYTES),
         name="consensus",
-    )(replicas, factor_seeds, edge_counts)
+    )(*(pltpu.with_memory_space_constraint(v, pltpu.HBM) for v in (replicas, factor_seeds, edge_counts)))
     chunks = 5
     return pl.pallas_call(
         outer,
@@ -322,6 +354,7 @@
         in_specs=[pl.BlockSpec(memory_space=pltpu.VMEM)] * 2,
         out_specs=pl.BlockSpec(memory_space=pl.ANY),
         scratch_shapes=[pltpu.VMEM((chunks, rows, width // chunks), f32), dma((chunks,))],
+        compiler_params=pltpu.CompilerParams(vmem_limit_bytes=VMEM_BYTES),
         name="outer",
     )(left, right)
 

time: 76.1 us -> 68.4 us (0.90)
  Pallas kernels: 72.3 us -> 67.8 us
  local copies, waits for them, and re-layouts: 2.93 us -> 0 us
    pallas_call x1, Pallas kernels: 69.3 us -> 65.8 us  [per_device(): pl.pallas_call(consensus, out_shape=[jax.ShapeDtypeStruct((both, rows), f...]
    unnamed x2 -> x0, local copies, waits for them, and re-layouts: 2.93 us -> none
    pallas_call x1, Pallas kernels: 2.94 us -> 2.02 us  [per_device(): pl.pallas_call(outer, out_shape=jax.ShapeDtypeStruct((rows, width), f32),...]
where the time goes in v2:
time: 68.4 us; the launch traced here: 67.8 us
  Pallas kernels  67.8 us (99%)
    pallas_call x1, Pallas kernels, per_device(): pl.pallas_call(consensus, out_shape=[jax.ShapeDtypeStruct((both, rows), f...  65.8 us
    pallas_call x1, Pallas kernels, per_device(): pl.pallas_call(outer, out_shape=jax.ShapeDtypeStruct((rows, width), f32),...  2.02 us

profile of v2, /device:TPU:1, one launch (start us, length us, event | category | flops | bytes accessed | tf_op | source)
XLA Modules:
  0.0 67.8 jit_solution(2402674428752108049)
XLA Ops:
  0.0 65.8 %consensus.1 = (f32[16,320]{1,0:T(8,128)S(1)}, f32[16,2560]{1,0:T(8,128)S(1)}) custom-call(bf16[320,2560]{1,0:T(8,128)(2,1)} %x_hbm.1, s32[8,2,2,8]{3,2,1,0:T(2,128)} %bitcast.2, s32[8,2,8]{2,1,0:T(2,128)} %bitcast.3), custom_call_target="tpu_custom_call" | custom-call | tf_op jit(solution)/shard_map/consensus/pallas_call | solution.py:310
  65.8 2.0 %outer.1 = f32[320,2560]{1,0:T(8,128)} custom-call(f32[16,320]{1,0:T(8,128)S(1)} %get-tuple-element.7.left_ref, f32[16,2560]{1,0:T(8,128)S(1)} %get-tuple-element.8.right_ref), custom_call_target="tpu_custom_call" | custom-call | tf_op jit(solution)/shard_map/outer/pallas_call | solution.py:351
